TPU v7x, 256 devices: a whole 4x4x8 slice. The times are simulated.
256 devices in a mesh: gx: 8 (over z), gy: 4 (over x), gz: 8 (over y, core).
Axes of the slice: x: 4, y: 4, z: 8, core: 2. Of those that a mesh axis runs over, the one named last changes fastest.
Arguments:
- grads: float32 [256, 1, 1048576], P(('gx', 'gy', 'gz')), may hold values from -650 to 650
- loss_scale: float32 [], replicated, may hold values from 8 to 64
Outputs:
- clipped: float32 [1, 1048576], P(None, ('gx', 'gy', 'gz'))
- grad_norm: float32 [], replicated
All inputs are finite; a program needn't handle non-finite values.
Results may differ from a plain program's by a relative error of at most 0.00002.
Values sent between devices are 32-bit elements; how exact they have to be, the bound alone decides.
A program may use at most 64 MiB of HBM per device.

v0:
```python
import jax
import jax.numpy as jnp
from jax import lax
from jax.sharding import Mesh
from jax.sharding import PartitionSpec as P

GX_GY_GZ = ("gx", "gy", "gz_0", "gz_1")


def cut_along(array, dim, length):
    before, after = (array.shape[:dim], array.shape[dim + 1 :])
    return jnp.moveaxis(array.reshape(*before, length, -1, *after), dim, 0)


def sent_and_summed(array, axis, dim):
    length = lax.axis_size(axis)
    blocks = lax.all_to_all(cut_along(array, dim, length), axis, 0, 0, tiled=True)
    return jnp.sum(blocks, axis=0)


def sum_in_two_steps(array, axes, dim):
    far, near = axes
    own = sent_and_summed(cut_along(array, dim, lax.axis_size(far)), near, dim + 1)
    return jnp.sum(lax.all_to_all(own, far, 0, 0, tiled=True), axis=0)


def sent_to_all(array, axis):
    copies = jnp.broadcast_to(array, (lax.axis_size(axis), *array.shape))
    return lax.all_to_all(copies, axis, split_axis=0, concat_axis=0, tiled=True)


def over_copies(array, axis):
    return sent_to_all(array, axis).sum(axis=0)


def over_axes(array, axes):
    far, near = axes
    return over_copies(over_copies(array, near), far)


def per_device(grads, loss_scale):
    local = grads[0]
    entries = local.shape[0] * local.shape[1]
    mine = sum_in_two_steps(local, (("gx", "gy"), ("gz_0", "gz_1")), 1) / loss_scale
    square = over_axes(jnp.sum(mine * mine), (("gx", "gy"), ("gz_0", "gz_1")))
    grad_norm = jnp.sqrt(square)
    factor = jnp.minimum(1.0, 0.5 * jnp.sqrt(jnp.float32(entries)) / (grad_norm + 1e-06))
    return (mine * factor, grad_norm)


def solution(mesh):
    torus = Mesh(
        mesh.devices.reshape(mesh.shape["gx"], mesh.shape["gy"], 4, 2), ("gx", "gy", "gz_0", "gz_1")
    )
    placed = (P(GX_GY_GZ, None, None), P())
    return jax.shard_map(
        per_device, mesh=torus, in_specs=placed, out_specs=(P(None, GX_GY_GZ), P()), check_vma=False
    )
```

profile of v0, /device:TPU:1, one launch (start us, length us, event | category | flops | bytes accessed | tf_op | source)
XLA Modules:
  0.0 123.0 jit_solution(956699849181283893)
XLA Ops:
  0.6 6.0 %copy.13 = f32[1,1,256,4096]{3,2,1,0:T(8,128)S(1)} copy(f32[1,1,256,4096]{3,1,2,0:T(1,128)} %bitcast.12) | data formatting | bytes 8388608
  6.6 2.4 %copy.6 = f32[8,32,1,4096]{3,1,2,0:T(8,128)S(1)} copy(f32[8,32,1,4096]{3,0,1,2:T(8,128)S(1)} %bitcast.11) | data formatting | bytes 8388608 | tf_op jit(solution)/shard_map/transpose | solution.py:12
  9.0 55.1 %all_to_all.22 = f32[8,32,1,4096]{3,1,2,0:T(8,128)} all-to-all(f32[8,32,1,4096]{3,1,2,0:T(8,128)S(1)} %copy.6), channel_id=1, replica_groups=mesh['gx'=8,'gy'=4,'gz_0'=4,'gz_1'=2] {'gz_0','gz_1'}, dimensions={0} | all-to-all | bytes 8388608 | tf_op jit(solution)/shard_map/all_to_all | solution.py:17
  64.1 2.4 %reduce_sum.47 = f32[32,4096]{1,0:T(8,128)S(1)} reduce(f32[8,32,1,4096]{3,1,2,0:T(8,128)} %all_to_all.22, f32[]{:T(128)} %constant.0.clone.1), dimensions={0,2}, to_apply=%region_0.0 | reduce | flops 917504 | bytes 4718596 | tf_op jit(solution)/shard_map/reduce_sum | solution.py:18
  66.6 1.4 %reduce_sum.48 = f32[32,1,4096]{2,1,0:T(1,128)} reshape(f32[32,4096]{1,0:T(8,128)S(1)} %reduce_sum.47) | data formatting | bytes 1048576 | tf_op jit(solution)/shard_map/reduce_sum | solution.py:18
  68.0 10.5 %all-to-all-start.1 = ((f32[32,1,4096]{2,1,0:T(1,128)}), f32[32,1,4096]{2,1,0:T(1,128)S(1)}, u32[]{:S(2)}, u32[]{:S(2)}) async-start(f32[32,1,4096]{2,1,0:T(1,128)} %reduce_sum.48), calls=%async_computation.1 | async-start | bytes 1048576 | tf_op jit(solution)/shard_map/all_to_all | solution.py:24
  79.1 14.7 %all-to-all-done.1 = f32[32,1,4096]{2,1,0:T(1,128)S(1)} async-done(((f32[32,1,4096]{2,1,0:T(1,128)}), f32[32,1,4096]{2,1,0:T(1,128)S(1)}, u32[]{:S(2)}, u32[]{:S(2)}) %all-to-all-start.1) | async-done | bytes 524320 | tf_op jit(solution)/shard_map/all_to_all | solution.py:24
  93.7 0.4 reduce_sum.49
  94.1 0.6 multiply_reduce_fusion
  94.7 0.6 broadcast_in_dim.6
  95.4 10.5 %all_to_all.23 = f32[8,1,1]{2,1,0:T(1,128)S(1)} all-to-all(f32[8,1,1]{2,1,0:T(1,128)S(1)} %broadcast_in_dim.6), channel_id=1, replica_groups=mesh['gx'=8,'gy'=4,'gz_0'=4,'gz_1'=2] {'gz_0','gz_1'}, dimensions={0} | all-to-all | bytes 64 | tf_op jit(solution)/shard_map/all_to_all | solution.py:29
  105.9 0.6 reduce_sum.51
  106.5 0.7 broadcast_in_dim.7
  107.2 12.8 %all_to_all.24 = f32[32,1,1]{2,1,0:T(1,128)S(1)} all-to-all(f32[32,1,1]{2,1,0:T(1,128)S(1)} %broadcast_in_dim.7), channel_id=1, replica_groups=mesh['gx'=8,'gy'=4,'gz_0'=4,'gz_1'=2] {'gx','gy'}, dimensions={0} | all-to-all | bytes 256 | tf_op jit(solution)/shard_map/all_to_all | solution.py:29
  119.9 0.6 reduce_sum.52
  121.3 0.6 broadcast_multiply_fusion
Async XLA Ops:
  68.0 25.8 %all-to-all-start.1 = ((f32[32,1,4096]{2,1,0:T(1,128)}), f32[32,1,4096]{2,1,0:T(1,128)S(1)}, u32[]{:S(2)}, u32[]{:S(2)}) async-start(f32[32,1,4096]{2,1,0:T(1,128)} %reduce_sum.48), calls=%async_computation.1 | async-start | bytes 1048576 | tf_op jit(solution)/shard_map/all_to_all | solution.py:24
where the time goes:
time: 123 us
  blocking collectives  78.4 us (64%)
  waiting for transfers between devices  14.7 us (12%)
  local copies, waits for them, and re-layouts  11.1 us (9%)
  starting transfers between devices  10.5 us (9%)
  other arithmetic  5.27 us (4%)
  between operations  3.18 us (3%)
    all_to_all x1, blocking collectives, sent_and_summed(): lax.all_to_all(cut_along(array, dim, length), axis, 0, 0, tiled=True)  55.1 us
    all_to_all x2, blocking collectives, sent_to_all(): return lax.all_to_all(copies, axis, split_axis=0, concat_axis=0, tiled=True)  23.3 us
    all_to_all x1, waiting for transfers between devices, sum_in_two_steps(): return jnp.sum(lax.all_to_all(own, far, 0, 0, tiled=True), axis=0)  14.7 us
    all_to_all x1, starting transfers between devices, sum_in_two_steps(): return jnp.sum(lax.all_to_all(own, far, 0, 0, tiled=True), axis=0)  10.5 us
    unnamed x1, local copies, waits for them, and re-layouts  5.98 us
  transfers between devices with their start and end apart: 1, of which 1 were waited for; matrix products, arithmetic and copies ran while one was open for 0% of the time, Pallas kernels for 0%

commit v1 on v0

v1 whole, which is shorter than its diff:
```python
import jax
import jax.numpy as jnp
from jax import lax
from jax.experimental import pallas as pl
from jax.experimental.pallas import tpu as pltpu
from jax.sharding import Mesh
from jax.sharding import PartitionSpec as P

AXES = ("gx", "gy", "gz_0", "gz_1")
MESH = pl.DeviceIdType.MESH
TILE = 8
LANES = 128
SHARE = 32
RING = 24
PLANE = SHARE - RING

BLOCKS = (
    ("p", 2, 2), ("p", 2, 3), ("c", 4), ("p", 2, 1), ("p", 2, 0), ("c", 3), ("c", 5),
    ("p", 1, 3), ("p", 3, 2), ("p", 1, 0), ("p", 3, 1), ("c", 2), ("c", 6),
    ("p", 1, 2), ("p", 3, 3), ("p", 1, 1), ("p", 3, 0), ("c", 1), ("c", 7),
    ("p", 0, 2), ("p", 0, 3), ("p", 0, 1), ("p", 0, 0), ("c", 0),
)


class Names:
    def __init__(self):
        self.numbers = {}

    def __getitem__(self, name):
        return self.numbers.setdefault(name, len(self.numbers))


MESSAGES = 112


def kernel(
    g, scale, out, norm,
    pown, ppeer, cown, cpeer, prp, prm, pdp, pdm, p2rp, p2rm, p2dp, p2dm, pt, p3, crp, crm, cpl,
    nrow, nplane, zrow, nz, load_sem, send_sem, recv_sem, plane_send, plane_recv,
):
    z, x, y, c = (lax.axis_index(a) for a in AXES)
    names = Names()
    pending = []

    def ring_at(u, v, core):
        return u + core * (v - u), v + core * (u - v)

    p, q = ring_at(x, y, c)
    other = 1 - c

    def copy(name, src, dst, device):
        n = names[name]
        return pltpu.make_async_remote_copy(
            src_ref=src, dst_ref=dst, send_sem=send_sem.at[n], recv_sem=recv_sem.at[n],
            device_id=device, device_id_type=MESH,
        )

    def send(name, src, dst, device):
        message = copy(name, src, dst, device)
        message.start()
        pending.append(message)

    def wait(name, dst):
        copy(name, dst, dst, (z, x, y, other)).wait_recv()

    def along(u, v, zz):
        xx, yy = ring_at(lax.rem(p + u, 4), lax.rem(q + v, 4), c)
        return (lax.rem(z + zz, 8), xx, yy, c)

    u_next, u_back = along(1, 0, 0), along(3, 0, 0)
    v_next, v_back = along(0, 1, 0), along(0, 3, 0)
    z_next, z_back = along(0, 0, 1), along(0, 0, 7)
    partner = (z, x, y, other)

    def source(block, core):
        if block[0] == "p":
            pp, qq = ring_at(x, y, core)
            xx, yy = ring_at(lax.rem(pp + block[1], 4), lax.rem(qq + block[2], 4), core)
            return g.at[:, xx, yy, core, pl.ds(0, RING)]
        return g.at[lax.rem(z + block[1], 8), :, :, core, pl.ds(RING, PLANE)]

    def place(block, first, second):
        return first.at[block[1], block[2]] if block[0] == "p" else second.at[block[1]]

    loads = {}
    for n, block in enumerate(BLOCKS):
        loads[block] = pltpu.make_async_copy(source(block, c), place(block, pown, cown), load_sem.at[n])
        loads[block].start()

    barrier = pltpu.get_barrier_semaphore()
    greeted = (partner, u_next, u_back, v_next, v_back, z_next, z_back)
    for device in greeted:
        pl.semaphore_signal(barrier, inc=1, device_id=device, device_id_type=MESH)
    pl.semaphore_wait(barrier, len(greeted))

    for block in BLOCKS:
        send(("core", block), source(block, other), place(block, ppeer, cpeer), partner)

    def both(block):
        loads[block].wait()
        wait(("core", block), place(block, ppeer, cpeer))
        if block[0] == "p":
            _, k, j = block
            pown[k, j] = pown[k, j] + ppeer[k, j]
        else:
            k = block[1]
            cown[k] = cown[k] + cpeer[k]

    def half(h):
        return pl.ds(2 * h, 2)

    def c_up(m, h):
        send(("c+", m, h), cown.at[5 - m, half(h)], crp.at[m - 1, half(h)], z_next)

    def c_down(m, h):
        send(("c-", m, h), cown.at[3 + m, half(h)], crm.at[m - 1, half(h)], z_back)

    def c_up_arrived(m, h):
        wait(("c+", m, h), crp.at[m - 1, half(h)])
        k = 4 - m
        cown[k, half(h)] = cown[k, half(h)] + crp[m - 1, half(h)]

    def c_down_arrived(m, h):
        wait(("c-", m, h), crm.at[m - 1, half(h)])
        k = (4 + m) % 8
        cown[k, half(h)] = cown[k, half(h)] + crm[m - 1, half(h)]

    def d_up(j):
        send(("d+", j), pown.at[1, j], pdp.at[j], u_next)

    def d_down(j):
        send(("d-", j), pown.at[3, j], pdm.at[j], u_back)

    def r_up(i, j):
        send(("r+", i), pown.at[2, j], prp.at[i], u_next)

    def r_down(i, j):
        send(("r-", i), pown.at[2, j], prm.at[i], u_back)

    after = {
        ("p", 2, 2): lambda: r_up(0, 2),
        ("p", 2, 3): lambda: r_down(0, 3),
        ("p", 2, 1): lambda: r_up(1, 1),
        ("p", 2, 0): lambda: r_down(1, 0),
        ("c", 4): lambda: (c_up(1, 0), c_down(1, 1)),
        ("c", 3): lambda: c_up(2, 1),
        ("c", 5): lambda: c_down(2, 0),
        ("p", 1, 3): lambda: d_up(3),
        ("p", 3, 2): lambda: d_down(2),
        ("p", 1, 0): lambda: d_up(0),
        ("p", 3, 1): lambda: d_down(1),
    }
    for block in BLOCKS:
        both(block)
        if block in after:
            after[block]()

    def c_relay(m):
        for h in (1, 0) if m > 1 else (0,):
            c_up_arrived(m, h)
            if m < 4:
                c_up(m + 1, h)
        for h in (0, 1) if m > 1 else (1,):
            c_down_arrived(m, h)
            if m < 4:
                c_down(m + 1, h)

    def r_relay(i, up, down):
        wait(("r+", i), prp.at[i])
        pown[1, up] = pown[1, up] + prp[i]
        d_up(up)
        wait(("r-", i), prm.at[i])
        pown[3, down] = pown[3, down] + prm[i]
        d_down(down)

    def ring_sum(j):
        wait(("d+", j), pdp.at[j])
        wait(("d-", j), pdm.at[j])
        pown[0, j] = pown[0, j] + pdp[j] + pdm[j]

    c_relay(1)
    r_relay(0, 2, 3)
    r_relay(1, 1, 0)
    c_relay(2)

    low, high = pl.ds(0, 4), pl.ds(4, 4)
    ring_sum(2)
    send(("r2+",), pown.at[0, 2, low], p2rp, v_next)
    send(("r2-",), pown.at[0, 2, high], p2rm, v_back)
    ring_sum(3)
    send(("d2-", 0), pown.at[0, 3, low], p2dm.at[low], v_back)
    ring_sum(1)
    send(("d2+", 1), pown.at[0, 1, high], p2dp.at[high], v_next)
    c_relay(3)
    ring_sum(0)
    wait(("r2+",), p2rp)
    pown[0, 1, low] = pown[0, 1, low] + p2rp[...]
    send(("d2+", 0), pown.at[0, 1, low], p2dp.at[low], v_next)
    wait(("r2-",), p2rm)
    pown[0, 3, high] = pown[0, 3, high] + p2rm[...]
    send(("d2-", 1), pown.at[0, 3, high], p2dm.at[high], v_back)
    c_relay(4)
    for h in (0, 1):
        part = (low, high)[h]
        wait(("d2+", h), p2dp.at[part])
        wait(("d2-", h), p2dm.at[part])
    pt[...] = pown[0, 0] + p2dp[...] + p2dm[...]

    for d in (4, 3, 5, 2, 6, 1, 7):
        target = along(0, 0, d)
        send(("z", d), pt.at[target[0]], p3.at[d], target)
    for a in range(4):
        for b in range(4):
            if a or b:
                xx, yy = lax.rem(x + a, 4), lax.rem(y + b, 4)
                send(("xy", a, b), cown.at[0, xx, yy], cpl.at[4 * a + b], (z, xx, yy, c))

    mine = cown[0, x, y]
    for a in range(4):
        for b in range(4):
            if a or b:
                wait(("xy", a, b), cpl.at[4 * a + b])
                mine = mine + cpl[4 * a + b]
    ours = pt[z]
    for d in (1, 7, 2, 6, 3, 5, 4):
        wait(("z", d), p3.at[d])
        ours = ours + p3[d]
    divisor = scale[0, 0]
    ours = ours / divisor
    mine = mine / divisor

    squares = mine * mine
    for t in range(RING // TILE):
        piece = ours[TILE * t : TILE * (t + 1)]
        squares = squares + piece * piece
    row = jnp.sum(squares, axis=0, keepdims=True)
    nrow[...] = row
    slot = 8 * x + 2 * y + c
    nplane[slot] = row
    for a in range(4):
        for b in range(4):
            for e in range(2):
                if a or b or e:
                    device = (z, lax.rem(x + a, 4), lax.rem(y + b, 4), lax.rem(c + e, 2))
                    message = pltpu.make_async_remote_copy(
                        src_ref=nrow, dst_ref=nplane.at[slot], send_sem=plane_send, recv_sem=plane_recv,
                        device_id=device, device_id_type=MESH,
                    )
                    message.start()
    others = nplane.at[pl.ds(0, 31)]
    pltpu.make_async_copy(others, others, plane_recv).wait()
    row = jnp.sum(nplane[...], axis=0)
    zrow[...] = row
    nz[z] = row
    for d in (4, 3, 5, 2, 6, 1, 7):
        target = along(0, 0, d)
        send(("nz", d), zrow, nz.at[z], target)
    for d in (1, 7, 2, 6, 3, 5, 4):
        wait(("nz", d), nz.at[lax.rem(z + 8 - d, 8)])
    total = jnp.sum(jnp.sum(nz[...], axis=0), axis=1, keepdims=True)
    length = jnp.sqrt(total)
    factor = jnp.minimum(1.0, 512.0 / (length + 1e-06))
    norm[...] = length
    out[0:RING] = ours * factor
    out[RING:SHARE] = mine * factor

    for message in pending:
        message.wait_send()
    pltpu.make_async_copy(others, others, plane_send).wait()
    assert len(names.numbers) <= MESSAGES, len(names.numbers)


def per_device(grads, loss_scale):
    blocks = grads.reshape(8, 4, 4, 2, SHARE, LANES)
    f32 = jnp.float32

    def vmem(*shape):
        return pltpu.VMEM((*shape, LANES), f32)

    clipped, norm = pl.pallas_call(
        kernel,
        name="reduce_clip",
        out_shape=(
            jax.ShapeDtypeStruct((SHARE, LANES), f32),
            jax.ShapeDtypeStruct((1, 1), f32),
        ),
        in_specs=[
            pl.BlockSpec(memory_space=pltpu.HBM),
            pl.BlockSpec(memory_space=pltpu.SMEM),
        ],
        out_specs=(
            pl.BlockSpec(memory_space=pltpu.VMEM),
            pl.BlockSpec(memory_space=pltpu.VMEM),
        ),
        scratch_shapes=[
            vmem(4, 4, 8, RING), vmem(4, 4, 8, RING),
            vmem(8, 4, 4, PLANE), vmem(8, 4, 4, PLANE),
            vmem(2, 8, RING), vmem(2, 8, RING),
            vmem(4, 8, RING), vmem(4, 8, RING),
            vmem(4, RING), vmem(4, RING),
            vmem(8, RING), vmem(8, RING),
            vmem(8, RING), vmem(8, RING),
            vmem(4, 4, 4, PLANE), vmem(4, 4, 4, PLANE),
            vmem(16, PLANE),
            vmem(1), vmem(32, 1), vmem(1), vmem(8, 1),
            pltpu.SemaphoreType.DMA((len(BLOCKS),)),
            pltpu.SemaphoreType.DMA((MESSAGES,)),
            pltpu.SemaphoreType.DMA((MESSAGES,)),
            pltpu.SemaphoreType.DMA,
            pltpu.SemaphoreType.DMA,
        ],
        compiler_params=pltpu.CompilerParams(collective_id=0, has_side_effects=True),
    )(blocks, loss_scale.reshape(1, 1))
    return clipped.reshape(1, SHARE * LANES), norm.reshape(())


def solution(mesh):
    torus = Mesh(mesh.devices.reshape(mesh.shape["gx"], mesh.shape["gy"], 4, 2), AXES)
    return jax.shard_map(
        per_device,
        mesh=torus,
        in_specs=(P(AXES, None, None), P()),
        out_specs=(P(None, AXES), P()),
        check_vma=False,
    )
```

time: 123 us -> 46.1 us (0.37)
  blocking collectives: 78.4 us -> 0 us
  Pallas kernels: 0 us -> 41.5 us
  waiting for transfers between devices: 14.7 us -> 0 us
  starting transfers between devices: 10.5 us -> 0 us
  local copies, waits for them, and re-layouts: 11.1 us -> 1.32 us
  other arithmetic: 5.27 us -> 0 us
    all_to_all x3 -> x0, blocking collectives: 78.4 us -> none  [the longest x1 55.1 us: sent_and_summed(): lax.all_to_all(cut_along(array, dim, length), axis, 0, 0, tiled=True)]
    pallas_call x0 -> x1, Pallas kernels: none -> 41.5 us  [per_device(): pl.pallas_call(kernel, name='reduce_clip', out_shape=(jax.ShapeDtypeStruc...]
    all_to_all x1 -> x0, waiting for transfers between devices: 14.7 us -> none  [sum_in_two_steps(): return jnp.sum(lax.all_to_all(own, far, 0, 0, tiled=True), axis=0)]
    all_to_all x1 -> x0, starting transfers between devices: 10.5 us -> none  [sum_in_two_steps(): return jnp.sum(lax.all_to_all(own, far, 0, 0, tiled=True), axis=0)]
    unnamed x1, local copies, waits for them, and re-layouts: 5.98 us -> 1.32 us
    reduce_sum x5 -> x0, other arithmetic: 4.65 us -> none  [the longest x1 2.45 us: sent_and_summed(): return jnp.sum(blocks, axis=0)]
    transpose x1 -> x0, local copies, waits for them, and re-layouts: 2.43 us -> none  [cut_along(): return jnp.moveaxis(array.reshape(*before, length, -1, *after), dim, 0)]
    reduce_sum x1 -> x0, local copies, waits for them, and re-layouts: 1.36 us -> none  [sent_and_summed(): return jnp.sum(blocks, axis=0)]
  transfers between devices with their start and end apart: 1 -> 0, of which waited for: 1 -> 0; matrix products, arithmetic and copies ran while one was open for 0% -> 0% of each run, Pallas kernels for 0% -> 0%
where the time goes in v1:
time: 46.1 us; the launch traced here: 45.9 us
  Pallas kernels  41.5 us (90%)
  between operations  3.05 us (7%)
  local copies, waits for them, and re-layouts  1.32 us (3%)
    pallas_call x1, Pallas kernels, per_device(): pl.pallas_call(kernel, name='reduce_clip', out_shape=(jax.ShapeDtypeStruc...  41.5 us
    unnamed x1, local copies, waits for them, and re-layouts  1.32 us

profile of v1, /device:TPU:1, one launch (start us, length us, event | category | flops | bytes accessed | tf_op | source)
XLA Modules:
  0.0 45.9 jit_solution(16971241796314248308)
XLA Ops:
  1.3 41.5 %reduce_clip.1 = (f32[32,128]{1,0:T(8,128)}, f32[1,1]{1,0:T(1,128)}) custom-call(f32[8,4,4,2,32,128]{5,4,3,2,1,0:T(8,128)} %bitcast.5, f32[1,1]{1,0:T(1,128)} %bitcast.4.scale), custom_call_target="tpu_custom_call" | custom-call | tf_op jit(solution)/shard_map/reduce_clip/pallas_call | solution.py:280
  42.8 1.3 %copy.7 = f32[1,4096]{1,0:T(1,128)} copy(f32[1,4096]{1,0:T(1,128)} %bitcast.6) | data formatting | bytes 32768

commit v2 on v1

--- a/solution.py
+++ b/solution.py
@@ -30,17 +30,21 @@
         return self.numbers.setdefault(name, len(self.numbers))
 
 
-MESSAGES = 112
+MESSAGES = 64
+EACH = ("core", "r+", "r-", "d+", "d-", "c+", "c-", "r2+", "r2-", "d2+", "d2-")
+SENT = (
+    ("corep",), ("corec",), ("r+", "r-", "d+", "d-"), ("c+", "c-"), ("r2+", "r2-", "d2+", "d2-"), ("z",), ("xy",), ("nz",), ("plane",),
+)
 
 
 def kernel(
-    g, scale, out, norm,
+    g, scale, out, norm, scaled,
     pown, ppeer, cown, cpeer, prp, prm, pdp, pdm, p2rp, p2rm, p2dp, p2dm, pt, p3, crp, crm, cpl,
-    nrow, nplane, zrow, nz, load_sem, send_sem, recv_sem, plane_send, plane_recv,
+    nrow, nplane, zrow, nz, load_sem, send_sem, recv_sem,
 ):
     z, x, y, c = (lax.axis_index(a) for a in AXES)
     names = Names()
-    pending = []
+    kinds = {kind: n for n, group in enumerate(SENT) for kind in group}
 
     def ring_at(u, v, core):
         return u + core * (v - u), v + core * (u - v)
@@ -49,16 +53,21 @@
     other = 1 - c
 
     def copy(name, src, dst, device):
-        n = names[name]
+        n = names[name if name[0] in EACH else name[:1]]
+        kind = kinds[name[0] + name[1][0] if name[0] == "core" else name[0]]
         return pltpu.make_async_remote_copy(
-            src_ref=src, dst_ref=dst, send_sem=send_sem.at[n], recv_sem=recv_sem.at[n],
+            src_ref=src, dst_ref=dst, send_sem=send_sem.at[kind], recv_sem=recv_sem.at[n],
             device_id=device, device_id_type=MESH,
         )
 
     def send(name, src, dst, device):
-        message = copy(name, src, dst, device)
-        message.start()
-        pending.append(message)
+        copy(name, src, dst, device).start()
+
+    def arrived(name, whole):
+        pltpu.make_async_copy(whole, whole, recv_sem.at[names[name]]).wait()
+
+    def sent(kind, whole):
+        pltpu.make_async_copy(whole, whole, send_sem.at[kinds[kind]]).wait()
 
     def wait(name, dst):
         copy(name, dst, dst, (z, x, y, other)).wait_recv()
@@ -82,10 +91,8 @@
     def place(block, first, second):
         return first.at[block[1], block[2]] if block[0] == "p" else second.at[block[1]]
 
-    loads = {}
-    for n, block in enumerate(BLOCKS):
-        loads[block] = pltpu.make_async_copy(source(block, c), place(block, pown, cown), load_sem.at[n])
-        loads[block].start()
+    for block in BLOCKS:
+        pltpu.make_async_copy(source(block, c), place(block, pown, cown), load_sem.at[int(block[0] == "c")]).start()
 
     barrier = pltpu.get_barrier_semaphore()
     greeted = (partner, u_next, u_back, v_next, v_back, z_next, z_back)
@@ -97,7 +104,6 @@
         send(("core", block), source(block, other), place(block, ppeer, cpeer), partner)
 
     def both(block):
-        loads[block].wait()
         wait(("core", block), place(block, ppeer, cpeer))
         if block[0] == "p":
             _, k, j = block
@@ -150,6 +156,8 @@
         ("p", 1, 0): lambda: d_up(0),
         ("p", 3, 1): lambda: d_down(1),
     }
+    pltpu.make_async_copy(pown, pown, load_sem.at[0]).wait()
+    pltpu.make_async_copy(cown, cown, load_sem.at[1]).wait()
     for block in BLOCKS:
         both(block)
         if block in after:
@@ -215,19 +223,21 @@
                 xx, yy = lax.rem(x + a, 4), lax.rem(y + b, 4)
                 send(("xy", a, b), cown.at[0, xx, yy], cpl.at[4 * a + b], (z, xx, yy, c))
 
+    arrived(("xy",), cpl.at[pl.ds(1, 15)])
     mine = cown[0, x, y]
     for a in range(4):
         for b in range(4):
             if a or b:
-                wait(("xy", a, b), cpl.at[4 * a + b])
                 mine = mine + cpl[4 * a + b]
+    arrived(("z",), p3.at[pl.ds(1, 7)])
     ours = pt[z]
     for d in (1, 7, 2, 6, 3, 5, 4):
-        wait(("z", d), p3.at[d])
         ours = ours + p3[d]
     divisor = scale[0, 0]
     ours = ours / divisor
     mine = mine / divisor
+    out[0:RING] = ours
+    out[RING:SHARE] = mine
 
     squares = mine * mine
     for t in range(RING // TILE):
@@ -242,31 +252,31 @@
             for e in range(2):
                 if a or b or e:
                     device = (z, lax.rem(x + a, 4), lax.rem(y + b, 4), lax.rem(c + e, 2))
-                    message = pltpu.make_async_remote_copy(
-                        src_ref=nrow, dst_ref=nplane.at[slot], send_sem=plane_send, recv_sem=plane_recv,
-                        device_id=device, device_id_type=MESH,
-                    )
-                    message.start()
+                    send(("plane",), nrow, nplane.at[slot], device)
     others = nplane.at[pl.ds(0, 31)]
-    pltpu.make_async_copy(others, others, plane_recv).wait()
+    arrived(("plane",), others)
     row = jnp.sum(nplane[...], axis=0)
     zrow[...] = row
     nz[z] = row
     for d in (4, 3, 5, 2, 6, 1, 7):
         target = along(0, 0, d)
         send(("nz", d), zrow, nz.at[z], target)
-    for d in (1, 7, 2, 6, 3, 5, 4):
-        wait(("nz", d), nz.at[lax.rem(z + 8 - d, 8)])
+    arrived(("nz",), nz.at[pl.ds(0, 7)])
     total = jnp.sum(jnp.sum(nz[...], axis=0), axis=1, keepdims=True)
     length = jnp.sqrt(total)
     factor = jnp.minimum(1.0, 512.0 / (length + 1e-06))
     norm[...] = length
-    out[0:RING] = ours * factor
-    out[RING:SHARE] = mine * factor
-
-    for message in pending:
-        message.wait_send()
-    pltpu.make_async_copy(others, others, plane_send).wait()
+    scaled[...] = jnp.broadcast_to(factor, (1, LANES))
+
+    sent("corep", ppeer)
+    sent("corec", cpeer)
+    sent("r+", pown.at[pl.ds(0, 3)])
+    sent("c+", cown.at[pl.ds(0, 7)])
+    sent("r2+", pown.at[0, pl.ds(0, 3)])
+    sent("z", p3.at[pl.ds(1, 7)])
+    sent("xy", cpl.at[pl.ds(1, 15)])
+    sent("plane", others)
+    sent("nz", nz.at[pl.ds(0, 7)])
     assert len(names.numbers) <= MESSAGES, len(names.numbers)
 
 
@@ -277,21 +287,15 @@
     def vmem(*shape):
         return pltpu.VMEM((*shape, LANES), f32)
 
-    clipped, norm = pl.pallas_call(
+    unscaled, norm, factor = pl.pallas_call(
         kernel,
         name="reduce_clip",
-        out_shape=(
-            jax.ShapeDtypeStruct((SHARE, LANES), f32),
-            jax.ShapeDtypeStruct((1, 1), f32),
-        ),
+        out_shape=(vmem(SHARE), pltpu.VMEM((1, 1), f32), vmem(1)),
         in_specs=[
             pl.BlockSpec(memory_space=pltpu.HBM),
             pl.BlockSpec(memory_space=pltpu.SMEM),
         ],
-        out_specs=(
-            pl.BlockSpec(memory_space=pltpu.VMEM),
-            pl.BlockSpec(memory_space=pltpu.VMEM),
-        ),
+        out_specs=(pl.BlockSpec(memory_space=pltpu.VMEM),) * 3,
         scratch_shapes=[
             vmem(4, 4, 8, RING), vmem(4, 4, 8, RING),
             vmem(8, 4, 4, PLANE), vmem(8, 4, 4, PLANE),
@@ -303,15 +307,13 @@
             vmem(4, 4, 4, PLANE), vmem(4, 4, 4, PLANE),
             vmem(16, PLANE),
             vmem(1), vmem(32, 1), vmem(1), vmem(8, 1),
-            pltpu.SemaphoreType.DMA((len(BLOCKS),)),
+            pltpu.SemaphoreType.DMA((2,)),
+            pltpu.SemaphoreType.DMA((len(SENT),)),
             pltpu.SemaphoreType.DMA((MESSAGES,)),
-            pltpu.SemaphoreType.DMA((MESSAGES,)),
-            pltpu.SemaphoreType.DMA,
-            pltpu.SemaphoreType.DMA,
         ],
         compiler_params=pltpu.CompilerParams(collective_id=0, has_side_effects=True),
     )(blocks, loss_scale.reshape(1, 1))
-    return clipped.reshape(1, SHARE * LANES), norm.reshape(())
+    return (unscaled * factor).reshape(1, SHARE * LANES), norm.reshape(())
 
 
 def solution(mesh):

time: 46.1 us -> 42.4 us (0.920)
  Pallas kernels: 41.5 us -> 39.2 us
  local copies, waits for them, and re-layouts: 1.32 us -> 0 us
  other arithmetic: 0 us -> 0.61 us
  between operations: 3.05 us -> 2.45 us
    pallas_call x1, Pallas kernels: 41.5 us -> 39.2 us  [per_device(): pl.pallas_call(kernel, name='reduce_clip', out_shape=(vmem(SHARE), pltpu....]
    unnamed x1 -> x0, local copies, waits for them, and re-layouts: 1.32 us -> none
    mul x0 -> x1, other arithmetic: none -> 0.61 us  [per_device(): return ((unscaled * factor).reshape(1, SHARE * LANES), norm.reshape(()))]
where the time goes in v2:
time: 42.4 us; the launch traced here: 42.2 us
  Pallas kernels  39.2 us (92%)
  between operations  2.45 us (6%)
  other arithmetic  0.61 us (1%)
    pallas_call x1, Pallas kernels, per_device(): pl.pallas_call(kernel, name='reduce_clip', out_shape=(vmem(SHARE), pltpu....  39.2 us

profile of v2, /device:TPU:1, one launch (start us, length us, event | category | flops | bytes accessed | tf_op | source)
XLA Modules:
  0.0 42.2 jit_solution(10433677703544114914)
XLA Ops:
  1.3 39.2 %reduce_clip.1 = (f32[32,128]{1,0:T(8,128)S(1)}, f32[1,1]{1,0:T(1,128)S(1)}, f32[1,128]{1,0:T(1,128)S(1)}) custom-call(f32[8,4,4,2,32,128]{5,4,3,2,1,0:T(8,128)} %bitcast.7, f32[1,1]{1,0:T(1,128)} %bitcast.5.scale), custom_call_target="tpu_custom_call" | custom-call | tf_op jit(solution)/shard_map/reduce_clip/pallas_call | solution.py:290
  40.5 0.6 %broadcast_multiply_fusion = f32[32,128]{1,0:T(8,128)} fusion(f32[32,128]{1,0:T(8,128)S(1)} %get-tuple-element.5, f32[128]{0:T(128)S(1)} %bitcast.6), kind=kLoop, calls=%fused_computation | loop fusion | flops 4096 | bytes 33280 | tf_op jit(solution)/shard_map/mul | solution.py:316
